TPU v7x, 32 devices: a whole 2x2x4 slice. The times are simulated.
32 devices in a mesh: cx: 4 (over y, x), cy: 8 (over z, core).
Axes of the slice: x: 2, y: 2, z: 4, core: 2. Of those that a mesh axis runs over, the one named last changes fastest.
Arguments:
- queries: bfloat16 [7, 2048, 128], P(None, ('cx', 'cy')), may hold values from -8 to 8, as said below
- keys: bfloat16 [2048, 128], P(('cx', 'cy')), may hold values from -40 to 40, as said below
- values: bfloat16 [2048, 128], P(('cx', 'cy')), may hold values from -6 to 6
Outputs:
- attended: bfloat16 [7, 2048, 128], P(None, ('cx', 'cy'))
Inputs may be any that keep to these rules, and one draw needn't show every extreme that they name: `queries`: every query is noise of about unit size in each entry plus one common direction of length 4, the same for all heads and tokens. The keys of the first four prompt positions carry a large component along the queries' common direction, so they draw much of every query's attention; all other keys are noise of about unit size in each entry.
All inputs are finite; a program needn't handle non-finite values.
Results may differ from a plain program's by a relative error of at most 0.001.
Values may be sent and summed in bfloat16 or wider, within the bound.
A program may use at most 192 MiB of HBM per device.

v0:
```python
import jax
import jax.numpy as jnp
from jax import lax
from jax.sharding import PartitionSpec as P

masked = -1e30


def partner(block, axis, bit):
    count = lax.axis_size(axis)
    route = []
    for low in range(count):
        high = low | (1 << bit)
        if high != low and high < count:
            route += [(low, high), (high, low)]
    return lax.ppermute(block, axis, route)


def attend(state, piece, start, queries_flat, query_pos, last_pos):
    keys_piece, values_piece = piece

    def update(carry):
        peak, total, mixed = carry
        head = queries_flat.shape[1]
        scores = jnp.dot(queries_flat, keys_piece.T, preferred_element_type=jnp.float32) * head ** (
            -0.5
        )
        key_pos = start + jnp.arange(keys_piece.shape[0], dtype=jnp.int32)
        visible = key_pos[None, :] <= query_pos[:, None]
        scores = jnp.where(visible, scores, masked)
        fresh = jnp.maximum(peak, jnp.max(scores, axis=1))
        shrink = jnp.exp(peak - fresh)
        weights = jnp.where(visible, jnp.exp(scores - fresh[:, None]), 0.0)
        total = total * shrink + jnp.sum(weights, axis=1)
        mixed = mixed * shrink[:, None] + jnp.dot(
            weights, values_piece.astype(jnp.float32), precision=lax.Precision.HIGHEST
        )
        return (fresh, total, mixed)

    return lax.cond(start <= last_pos, update, lambda carry: carry, state)


def local(queries, keys, values):
    group, tokens, head = queries.shape
    queries_flat = queries.reshape(group * tokens, head)
    here = lax.axis_index(("cx", "cy"))
    first = here * tokens
    last_pos = first + tokens - 1
    query_pos = first + jnp.arange(group * tokens, dtype=jnp.int32) % tokens
    rows = group * tokens
    state = (
        jnp.full((rows,), masked, jnp.float32),
        jnp.zeros((rows,), jnp.float32),
        jnp.zeros((rows, head), jnp.float32),
    )

    def fold(carry, piece, start):
        return attend(carry, piece, start, queries_flat, query_pos, last_pos)

    state = fold(state, (keys, values), first)
    held = jnp.concatenate([keys, values], axis=1)
    levels = lax.axis_size(("cx", "cy")).bit_length() - 1
    for level in range(levels):
        width = 2**level
        upper = here // width % 2
        partner_first = (here // width + 1 - 2 * upper) * width * tokens
        received = partner(held, ("cx", "cy"), level)
        state = fold(state, (received[:, :head], received[:, head:]), partner_first)
        if level + 1 < levels:
            held = jnp.where(
                upper == 1,
                jnp.concatenate([received, held], axis=0),
                jnp.concatenate([held, received], axis=0),
            )
    peak, total, mixed = state
    return (mixed / total[:, None]).astype(jnp.bfloat16).reshape(group, tokens, head)


def solution(mesh):
    in_specs = (P(None, ("cx", "cy"), None), P(("cx", "cy"), None), P(("cx", "cy"), None))
    out_specs = P(None, ("cx", "cy"), None)
    return jax.shard_map(local, mesh=mesh, in_specs=in_specs, out_specs=out_specs, check_vma=False)
```

profile of v0, /device:TPU:31, one launch (start us, length us, event | category | flops | bytes accessed | tf_op | source)
XLA Modules:
  0.0 44.1 jit_solution(912751943433815241)
XLA Ops:
  0.0 0.7 %constant_dynamic-update-slice_fusion.1 = bf16[64,256]{1,0:T(8,128)(2,1)S(1)} fusion(bf16[64,128]{1,0:T(8,128)(2,1)} %param.16), kind=kLoop, calls=%fused_computation.89 | loop fusion | bytes 32768
  0.7 0.7 %constant_dynamic-update-slice_fusion = bf16[64,256]{1,0:T(8,128)(2,1)S(1)} fusion(bf16[64,256]{1,0:T(8,128)(2,1)S(1)} %constant_dynamic-update-slice_fusion.1, bf16[64,128]{1,0:T(8,128)(2,1)} %param.17), kind=kLoop, calls=%fused_computation.88 | loop fusion | bytes 32768 | tf_op jit(solution)/shard_map/concatenate | solution.py:61
  2.1 0.9 %collective-permute-done = bf16[64,256]{1,0:T(8,128)(2,1)S(1)} collective-permute-done((bf16[64,256]{1,0:T(8,128)(2,1)S(1)}, bf16[64,256]{1,0:T(8,128)(2,1)S(1)}, u32[]{:S(2)}, u32[]{:S(2)}) %collective-permute-start) | collective-permute-done | bytes 32800 | tf_op jit(solution)/shard_map/ppermute | solution.py:16
  3.2 2.9 %collective-permute-done.1 = bf16[128,256]{1,0:T(8,128)(2,1)S(1)} collective-permute-done((bf16[128,256]{1,0:T(8,128)(2,1)S(1)}, bf16[128,256]{1,0:T(8,128)(2,1)S(1)}, u32[]{:S(2)}, u32[]{:S(2)}) %collective-permute-start.1) | collective-permute-done | bytes 65568 | tf_op jit(solution)/shard_map/ppermute | solution.py:16
  6.3 8.5 %collective-permute-done.2 = bf16[256,256]{1,0:T(8,128)(2,1)S(1)} collective-permute-done((bf16[256,256]{1,0:T(8,128)(2,1)S(1)}, bf16[256,256]{1,0:T(8,128)(2,1)S(1)}, u32[]{:S(2)}, u32[]{:S(2)}) %collective-permute-start.2) | collective-permute-done | bytes 131104 | tf_op jit(solution)/shard_map/ppermute | solution.py:16
  15.3 4.3 %conditional.6 = (f32[448]{0:T(512)}, f32[448]{0:T(512)S(1)}, f32[448,128]{1,0:T(8,128)S(1)}) conditional(s32[]{:T(128)} %convert_element_type.32, () %tuple.44, (s32[]{:T(128)}, s32[448]{0:T(512)S(1)}, bf16[448,128]{1,0:T(8,128)(2,1)}, bf16[64,128]{1,0:T(8,128)(2,1)}, bf16[64,128]{1,0:T(8,128)(2,1)}) %tuple.89), branch_computations={%region_0.1_spmd, %region_1.4_spmd} | conditional | flops 51754816 | bytes 747036 | solution.py:40
  15.3 1.1 %fusion.52 = (f32[448]{0:T(512)S(1)}, f32[448,64]{0,1:T(8,128)S(1)}) fusion(bf16[448,128]{1,0:T(8,128)(2,1)} %get-tuple-element.127, bf16[64,128]{1,0:T(8,128)(2,1)} %get-tuple-element.128, s32[448]{0:T(512)S(1)} %get-tuple-element.126, s32[64]{0:T(128)S(1)} %iota_add_fusion), kind=kOutput, calls=%fused_computation.96 | convolution fusion | flops 7454272 | bytes 249600 | tf_op jit(solution)/shard_map/cond/branch_1_fun/dot_general | solution.py:25
  17.0 0.8 %fusion.1 = f32[448]{0:T(512)S(1)} fusion(f32[448,64]{0,1:T(8,128)S(1)} %get-tuple-element.215, f32[448]{0:T(512)} %get-tuple-element.235, s32[448]{0:T(512)S(1)} %get-tuple-element.126, s32[64]{0:T(128)S(1)} %iota_add_fusion), kind=kLoop, calls=%fused_computation.4 | loop fusion | flops 114240 | bytes 120320 | tf_op jit(solution)/shard_map/cond/branch_1_fun/reduce_sum | solution.py:34
  18.4 1.2 %convolution_add_fusion = f32[448,128]{1,0:T(8,128)S(1)} fusion(bf16[64,128]{1,0:T(8,128)(2,1)} %get-tuple-element.129, f32[448]{0:T(512)S(1)} %get-tuple-element.202, f32[448,64]{0,1:T(8,128)S(1)} %get-tuple-element.215, f32[448]{0:T(512)} %get-tuple-element.235, s32[448]{0:T(512)S(1)} %get-tuple-element.126, s32[64]{0:T(128)S(1)} %iota_add_fusion), kind=kOutput, calls=%fused_computation | convolution fusion | flops 44183552 | bytes 366080 | tf_op jit(solution)/shard_map/cond/branch_1_fun/dot_general | solution.py:35
  19.6 2.2 %collective-permute-done.3 = bf16[512,256]{1,0:T(8,128)(2,1)S(1)} collective-permute-done((bf16[512,256]{1,0:T(8,128)(2,1)S(1)}, bf16[512,256]{1,0:T(8,128)(2,1)S(1)}, u32[]{:S(2)}, u32[]{:S(2)}) %collective-permute-start.3) | collective-permute-done | bytes 262176 | tf_op jit(solution)/shard_map/ppermute | solution.py:16
  22.3 3.6 %conditional.7 = ((f32[448]{0:T(512)}, f32[448]{0:T(512)S(1)}, f32[448,128]{1,0:T(8,128)S(1)})) conditional(s32[]{:T(128)} %convert_element_type.31, (f32[448]{0:T(512)}, f32[448]{0:T(512)S(1)}, f32[448,128]{1,0:T(8,128)S(1)}) %conditional.6, (s32[]{:T(128)}, s32[448]{0:T(512)S(1)}, bf16[448,128]{1,0:T(8,128)(2,1)}, bf16[64,128]{1,0:T(8,128)(2,1)S(1)}, ...), branch_computations={%region_4.5_spmd, %region_5.8_spmd} | conditional | flops 51811264 | bytes 985380 | solution.py:40
  22.3 1.1 %fusion.53 = (f32[448]{0:T(512)S(1)}, f32[448,64]{0,1:T(8,128)S(1)}) fusion(bf16[448,128]{1,0:T(8,128)(2,1)} %get-tuple-element.133, bf16[64,128]{1,0:T(8,128)(2,1)S(1)} %get-tuple-element.134, s32[448]{0:T(512)S(1)} %get-tuple-element.132, s32[64]{0:T(128)S(1)} %iota_add_fusion.1), kind=kOutput, calls=%fused_computation.97 | convolution fusion | flops 7454272 | bytes 249600 | tf_op jit(solution)/shard_map/cond/branch_1_fun/dot_general | solution.py:25
  26.0 4.0 %conditional.8 = ((f32[448]{0:T(512)}, f32[448]{0:T(512)S(1)}, f32[448,128]{1,0:T(8,128)S(1)})) conditional(s32[]{:T(128)} %convert_element_type.30, (f32[448]{0:T(512)}, f32[448]{0:T(512)S(1)}, f32[448,128]{1,0:T(8,128)S(1)}) %get-tuple-element.266, (s32[]{:T(128)}, s32[448]{0:T(512)S(1)}, bf16[448,128]{1,0:T(8,128)(2,1)}, ...), branch_computations={%region_8.9_spmd, %region_9.12_spmd} | conditional | flops 103506944 | bytes 1363236 | solution.py:40
  26.0 1.2 %fusion.54 = (f32[448]{0:T(512)S(1)}, f32[448,128]{1,0:T(8,128)S(1)}) fusion(bf16[448,128]{1,0:T(8,128)(2,1)} %get-tuple-element.141, bf16[128,128]{1,0:T(8,128)(2,1)S(1)} %get-tuple-element.142, s32[448]{0:T(512)S(1)} %get-tuple-element.140, s32[128]{0:T(128)S(1)} %iota_add_fusion.2), kind=kOutput, calls=%fused_computation.98 | convolution fusion | flops 14908992 | bytes 380928 | tf_op jit(solution)/shard_map/cond/branch_1_fun/dot_general | solution.py:25
  30.0 4.1 %conditional.9 = ((f32[448]{0:T(512)}, f32[448]{0:T(512)S(1)}, f32[448,128]{1,0:T(8,128)S(1)})) conditional(s32[]{:T(128)} %convert_element_type.29, (f32[448]{0:T(512)}, f32[448]{0:T(512)S(1)}, f32[448,128]{1,0:T(8,128)S(1)}) %get-tuple-element.267, (s32[]{:T(128)}, s32[448]{0:T(512)S(1)}, bf16[448,128]{1,0:T(8,128)(2,1)}, ...), branch_computations={%region_12.13_spmd, %region_13.16_spmd} | conditional | flops 206898304 | bytes 2118948 | solution.py:40
  30.0 1.2 %fusion.55 = (f32[448]{0:T(512)S(1)}, f32[448,256]{1,0:T(8,128)S(1)}) fusion(bf16[448,128]{1,0:T(8,128)(2,1)} %get-tuple-element.149, bf16[256,128]{1,0:T(8,128)(2,1)S(1)} %get-tuple-element.150, s32[448]{0:T(512)S(1)} %get-tuple-element.148, s32[256]{0:T(256)S(1)} %iota_add_fusion.3), kind=kOutput, calls=%fused_computation.99 | convolution fusion | flops 29818432 | bytes 643584 | tf_op jit(solution)/shard_map/cond/branch_1_fun/dot_general | solution.py:25
  34.0 4.4 %conditional.10 = ((f32[448]{0:T(512)}, f32[448]{0:T(512)S(1)}, f32[448,128]{1,0:T(8,128)S(1)})) conditional(s32[]{:T(128)} %convert_element_type.28, (f32[448]{0:T(512)}, f32[448]{0:T(512)S(1)}, f32[448,128]{1,0:T(8,128)S(1)}) %get-tuple-element.268, (s32[]{:T(128)}, s32[448]{0:T(512)S(1)}, bf16[512,256]{1,0:T(8,128)(2,1)S(1)}, ...), branch_computations={%region_16.17_spmd, %region_17.20_spmd} | conditional | flops 413681024 | bytes 3631396 | solution.py:40
  34.1 1.3 %fusion.56 = (f32[448]{0:T(512)S(1)}, f32[448,512]{1,0:T(8,128)S(1)}) fusion(bf16[448,128]{1,0:T(8,128)(2,1)} %get-tuple-element.157, bf16[512,256]{1,0:T(8,128)(2,1)S(1)} %get-tuple-element.158, s32[448]{0:T(512)S(1)} %get-tuple-element.156, s32[512]{0:T(512)S(1)} %iota_add_fusion.4), kind=kOutput, calls=%fused_computation.100 | convolution fusion | flops 59637312 | bytes 1169152 | tf_op jit(solution)/shard_map/cond/branch_1_fun/dot_general | solution.py:25
  36.4 0.7 %multiply_add_fusion.3 = (f32[448]{0:T(512)S(1)}, f32[448]{0:T(512)S(1)}) fusion(f32[448]{0:T(512)S(1)} %fusion.30, f32[448]{0:T(512)S(1)} %get-tuple-element.159, f32[448]{0:T(512)} %get-tuple-element.154, f32[448]{0:T(512)S(1)} %max.13), kind=kLoop, calls=%fused_computation.64 | loop fusion | flops 1344 | bytes 10752 | tf_op jit(solution)/shard_map/cond/branch_1_fun/add | solution.py:34
  37.7 0.8 %convolution_add_fusion.4 = f32[448,128]{1,0:T(8,128)S(1)} fusion(f32[448,512]{1,0:T(8,128)S(1)} %get-tuple-element.223, f32[448]{0:T(512)S(1)} %max.13, s32[512]{0:T(512)S(1)} %iota_add_fusion.4, s32[448]{0:T(512)S(1)} %get-tuple-element.156, f32[448,128]{1,0:T(8,128)S(1)} %get-tuple-element.160, bf16[512,256]{1,0:T(8,128)(2,1)S(1)} %get-tuple-element.158, ...), kind=kOutput, calls=%fused_computation.55 | convolution fusion | flops 353124352 | bytes 1515520 | tf_op jit(solution)/shard_map/cond/branch_1_fun/dot_general | solution.py:35
  38.5 4.8 %conditional.11 = ((f32[448]{0:T(512)S(1)}, f32[448,128]{1,0:T(8,128)S(1)})) conditional(s32[]{:T(128)} %convert_element_type.27, (f32[448]{0:T(512)S(1)}, f32[448,128]{1,0:T(8,128)S(1)}) %tuple.50, (s32[]{:T(128)}, s32[448]{0:T(512)S(1)}, bf16[1024,256]{1,0:T(8,128)(2,1)S(1)}, bf16[448,128]{1,0:T(8,128)(2,1)}, f32[448]{0:T(512)}, ...), branch_computations={%region_20.21_spmd, %region_21.24_spmd} | conditional | flops 827246464 | bytes 6650652 | solution.py:40
  38.5 1.4 %fusion.57 = (f32[448]{0:T(512)S(1)}, f32[448,1024]{1,0:T(8,128)S(1)}) fusion(bf16[448,128]{1,0:T(8,128)(2,1)} %get-tuple-element.165, bf16[1024,256]{1,0:T(8,128)(2,1)S(1)} %get-tuple-element.166, s32[448]{0:T(512)S(1)} %get-tuple-element.164, s32[1024]{0:T(1024)S(1)} %iota_add_fusion.5), kind=kOutput, calls=%fused_computation.101 | convolution fusion | flops 119275072 | bytes 2219776 | tf_op jit(solution)/shard_map/cond/branch_1_fun/dot_general | solution.py:25
  41.9 1.4 %fusion.40 = f32[448,128]{1,0:T(8,128)S(1)} fusion(f32[448,1024]{1,0:T(8,128)S(1)} %get-tuple-element.225, f32[448]{0:T(512)S(1)} %max.14, s32[1024]{0:T(1024)S(1)} %iota_add_fusion.5, s32[448]{0:T(512)S(1)} %get-tuple-element.164, bf16[1024,256]{1,0:T(8,128)(2,1)S(1)} %get-tuple-element.166, f32[448,128]{1,0:T(8,128)S(1)} %get-tuple-element.167, ...), kind=kOutput, calls=%fused_computation.72 | convolution fusion | flops 706134016 | bytes 2566144 | tf_op jit(solution)/shard_map/cond/branch_1_fun/dot_general | solution.py:35
  43.3 0.8 %divide_convert_fusion = bf16[448,128]{1,0:T(8,128)(2,1)} fusion(f32[448,128]{1,0:T(8,128)S(1)} %get-tuple-element.200, f32[448]{0:T(512)S(1)} %get-tuple-element.201), kind=kLoop, calls=%fused_computation.85 | loop fusion | flops 114688 | bytes 345856 | tf_op jit(solution)/shard_map/convert_element_type | solution.py:76
  (43 shorter events, 14.9 us)
Async XLA Ops:
  1.4 1.5 %collective-permute-start = (bf16[64,256]{1,0:T(8,128)(2,1)S(1)}, bf16[64,256]{1,0:T(8,128)(2,1)S(1)}, u32[]{:S(2)}, u32[]{:S(2)}) collective-permute-start(bf16[64,256]{1,0:T(8,128)(2,1)S(1)} %constant_dynamic-update-slice_fusion), channel_id=1, source_target_pairs={{0,1},{1,0},{2,3},{3,2},{4,5},{5,4},{6,7},{7,6},{8,9},{9,8},{10,11... | collective-permute-start | bytes 98312 | tf_op jit(solution)/shard_map/ppermute | solution.py:16
  3.0 3.2 %collective-permute-start.1 = (bf16[128,256]{1,0:T(8,128)(2,1)S(1)}, bf16[128,256]{1,0:T(8,128)(2,1)S(1)}, u32[]{:S(2)}, u32[]{:S(2)}) collective-permute-start(bf16[128,256]{1,0:T(8,128)(2,1)S(1)} %maximum_select_fusion.3), channel_id=1, source_target_pairs={{0,2},{2,0},{1,3},{3,1},{4,6},{6,4},{5,7},{7,5},{8,10},{10,8},{9,1... | collective-permute-start | bytes 196616 | tf_op jit(solution)/shard_map/ppermute | solution.py:16
  6.2 8.6 %collective-permute-start.2 = (bf16[256,256]{1,0:T(8,128)(2,1)S(1)}, bf16[256,256]{1,0:T(8,128)(2,1)S(1)}, u32[]{:S(2)}, u32[]{:S(2)}) collective-permute-start(bf16[256,256]{1,0:T(8,128)(2,1)S(1)} %maximum_select_fusion.2), channel_id=1, source_target_pairs={{0,4},{4,0},{1,5},{5,1},{2,6},{6,2},{3,7},{7,3},{8,12},{12,8},{9,1... | collective-permute-start | bytes 393224 | tf_op jit(solution)/shard_map/ppermute | solution.py:16
  14.9 6.9 %collective-permute-start.3 = (bf16[512,256]{1,0:T(8,128)(2,1)S(1)}, bf16[512,256]{1,0:T(8,128)(2,1)S(1)}, u32[]{:S(2)}, u32[]{:S(2)}) collective-permute-start(bf16[512,256]{1,0:T(8,128)(2,1)S(1)} %maximum_select_fusion.1), channel_id=1, source_target_pairs={{0,8},{8,0},{1,9},{9,1},{2,10},{10,2},{3,11},{11,3},{4,12},{12,4},... | collective-permute-start | bytes 786440 | tf_op jit(solution)/shard_map/ppermute | solution.py:16
  22.0 16.5 %collective-permute-start.4 = (bf16[1024,256]{1,0:T(8,128)(2,1)S(1)}, bf16[1024,256]{1,0:T(8,128)(2,1)S(1)}, u32[]{:S(2)}, u32[]{:S(2)}) collective-permute-start(bf16[1024,256]{1,0:T(8,128)(2,1)S(1)} %maximum_select_fusion), channel_id=1, source_target_pairs={{0,16},{16,0},{1,17},{17,1},{2,18},{18,2},{3,19},{19,3},{4,20},{20... | collective-permute-start | bytes 1572872 | tf_op jit(solution)/shard_map/ppermute | solution.py:16
where the time goes:
time: 44.8 us; the launch traced here: 44.1 us
  waiting for transfers between devices  14.5 us (32%)
  matrix products  12.2 us (27%)
  other arithmetic  11.7 us (26%)
  local copies, waits for them, and re-layouts  3.8 us (8%)
  starting transfers between devices  1.64 us (4%)
    ppermute x5, waiting for transfers between devices, partner(): return lax.ppermute(block, axis, route)  14.5 us
    dot_general x6, matrix products, update(): jnp.dot(queries_flat, keys_piece.T, preferred_element_type=jnp.float32)  7.36 us
    dot_general x6, matrix products, update(): jnp.dot(weights, values_piece.astype(jnp.float32), precision=lax.Precisio...  4.84 us
    add x6, other arithmetic, update(): total = total * shrink + jnp.sum(weights, axis=1)  4.18 us
    max x5, other arithmetic, update(): fresh = jnp.maximum(peak, jnp.max(scores, axis=1))  3.45 us
    reduce_sum x6, other arithmetic, update(): total = total * shrink + jnp.sum(weights, axis=1)  2.34 us
    cond x4, local copies, waits for them, and re-layouts  2.33 us
    ppermute x5, starting transfers between devices, partner(): return lax.ppermute(block, axis, route)  1.64 us
  transfers between devices with their start and end apart: 5, of which 4 were waited for; matrix products, arithmetic and copies ran while one was open for 46% of the time, Pallas kernels for 0%

commit v1 on v0

v1 whole, which is shorter than its diff:
```python
import functools

import jax
import jax.numpy as jnp
from jax import lax
from jax.experimental import pallas as pl
from jax.experimental.pallas import tpu as pltpu
from jax.sharding import PartitionSpec as P

MESH = pl.DeviceIdType.MESH
LOG2E = 1.4426950408889634
CORES = 2
SPAN = 8


def kernel(
    rows_n, line_n, queries_hbm, keys_hbm, values_hbm, out_ref,
    queries, kv, peak, total, mixed,
    in_sems, line_send, column_send, cross_send, mate_send, recv_sems,
):
    group, tokens, head = queries.shape
    count = group * tokens
    chips = line_n // CORES
    row = lax.axis_index("cx")
    place = lax.axis_index("cy")
    z, core = place // CORES, place % CORES
    mine = row * line_n + place
    cross_row = rows_n - 1 - row

    def block_id(r, zz, cc):
        return r * line_n + zz * CORES + cc

    def remote(block, sem, r, y):
        return pltpu.make_async_remote_copy(
            src_ref=kv.at[block], dst_ref=kv.at[block], send_sem=sem, recv_sem=recv_sems.at[block],
            device_id=(r, y), device_id_type=MESH,
        )

    def place_of(zz):
        return zz * CORES + core

    mate = z * CORES + 1 - core

    def to_line(block, sem, zz):
        return remote(block, sem, row, place_of(zz))

    def to_row(block, sem, r):
        return remote(block, sem, r, place)

    def to_mate(block):
        return remote(block, mate_send.at[block], row, mate)

    def arrived(block):
        to_mate(block).wait_recv()

    load_k = pltpu.make_async_copy(keys_hbm, kv.at[mine, 0], in_sems.at[0])
    load_v = pltpu.make_async_copy(values_hbm, kv.at[mine, 1], in_sems.at[1])
    load_q = pltpu.make_async_copy(queries_hbm, queries, in_sems.at[2])
    load_k.start()
    load_v.start()
    load_q.start()

    barrier = pltpu.get_barrier_semaphore()

    def greet_line(i, _):
        @pl.when(i != z)
        def _():
            pl.semaphore_signal(barrier, inc=1, device_id=(row, place_of(i)), device_id_type=MESH)
        return 0

    def greet_column(i, _):
        @pl.when(i != row)
        def _():
            pl.semaphore_signal(barrier, inc=1, device_id=(i, place), device_id_type=MESH)
        return 0

    lax.fori_loop(0, chips, greet_line, 0)
    lax.fori_loop(0, rows_n, greet_column, 0)
    pl.semaphore_signal(barrier, inc=1, device_id=(row, mate), device_id_type=MESH)
    load_k.wait()
    load_v.wait()
    pl.semaphore_wait(barrier, chips - 1 + rows_n - 1 + 1)

    def around(body):
        def step(d, _):
            @pl.when(z + d < chips)
            def _():
                body(z + d)

            @pl.when(z - d >= 0)
            def _():
                body(z - d)
            return 0

        lax.fori_loop(1, chips, step, 0)

    def later_rows(body):
        def step(r, _):
            body(r)
            return 0

        lax.fori_loop(row + 1, rows_n, step, 0)

    last_row = row == rows_n - 1
    has_cross = cross_row < row

    def send_own(zz):
        @pl.when(jnp.logical_or(zz > z, row < rows_n - 1))
        def _():
            to_line(mine, line_send.at[zz], zz).start()

    around(send_own)
    later_rows(lambda r: to_row(mine, column_send.at[r * chips + z], r).start())

    @pl.when(core == 0)
    def _():
        to_mate(mine).start()

    load_q.wait()
    scale = head ** (-0.5) * LOG2E

    def scores_of(first, blocks):
        k = kv[pl.ds(first, blocks), 0].reshape(blocks * tokens, head)
        q = queries[...].reshape(count, head)
        return lax.dot_general(q, k, (((1,), (1,)), ((), ())), preferred_element_type=jnp.float32)

    def mix(weights, first, blocks):
        v = kv[pl.ds(first, blocks), 1].reshape(blocks * tokens, head)
        high = weights.astype(jnp.bfloat16)
        low = (weights - high.astype(jnp.float32)).astype(jnp.bfloat16)
        return jnp.dot(high, v, preferred_element_type=jnp.float32) + jnp.dot(
            low, v, preferred_element_type=jnp.float32
        )

    def fold(first, blocks):
        scores = scores_of(first, blocks)
        old = peak[...]
        fresh = jnp.maximum(old, jnp.max(scores, axis=1, keepdims=True))
        shrink = jnp.exp2((old - fresh) * scale)
        weights = jnp.exp2((scores - fresh[:, :1]) * scale)
        peak[...] = fresh
        total[...] = total[...] * shrink + jnp.sum(weights, axis=1, keepdims=True)
        mixed[...] = mixed[...] * shrink + mix(weights, first, blocks)

    scores = scores_of(mine, 1)
    query_pos = lax.broadcasted_iota(jnp.int32, (count, tokens), 0) % tokens
    key_pos = lax.broadcasted_iota(jnp.int32, (count, tokens), 1)
    visible = key_pos <= query_pos
    scores = jnp.where(visible, scores, -1e30)
    top = jnp.max(scores, axis=1, keepdims=True)
    weights = jnp.where(visible, jnp.exp2((scores - top) * scale), 0.0)
    peak[...] = jnp.broadcast_to(top, peak.shape)
    total[...] = jnp.broadcast_to(jnp.sum(weights, axis=1, keepdims=True), total.shape)
    mixed[...] = mix(weights, mine, 1)

    def pass_own_row(zz):
        @pl.when(jnp.logical_or(zz < z, row < rows_n - 1))
        def _():
            block = block_id(row, zz, core)
            arrived(block)

            def on(r):
                @pl.when(r != cross_row)
                def _():
                    to_row(block, column_send.at[r * chips + zz], r).start()

            later_rows(on)

            @pl.when(zz < z)
            def _():
                to_mate(block).start()

    def pass_cross():
        block = block_id(cross_row, z, core)
        arrived(block)
        around(lambda zz: to_line(block, cross_send.at[zz], zz).start())
        to_mate(block).start()

    @pl.when(has_cross)
    def _():
        pass_cross()

    around(pass_own_row)

    @pl.when(core == 1)
    def _():
        block = block_id(row, z, 0)
        arrived(block)
        fold(block, 1)

    def own_row_step(zz, _):
        arrived(block_id(row, zz, 1 - core))
        fold(block_id(row, zz, 0), CORES)
        return 0

    lax.fori_loop(0, z, own_row_step, 0)

    def take_row(r):
        def step(zz):
            block = block_id(r, zz, core)
            arrived(block)
            to_mate(block).start()

        @pl.when(r != cross_row)
        def _():
            step(z)

        around(step)

    def fold_row(r):
        def wait_mate(zz, _):
            arrived(block_id(r, zz, 1 - core))
            return 0

        lax.fori_loop(0, chips, wait_mate, 0)
        span = min(SPAN, line_n)

        def part(i, _):
            fold(r * line_n + i * span, span)
            return 0

        lax.fori_loop(0, line_n // span, part, 0)

    def earlier(i, _):
        r = row - 1 - i
        take_row(r)
        fold_row(r)
        return 0

    lax.fori_loop(0, row, earlier, 0)

    out_ref[...] = (mixed[...] / total[...]).astype(out_ref.dtype).reshape(out_ref.shape)

    def sent_own(zz):
        @pl.when(jnp.logical_or(zz > z, row < rows_n - 1))
        def _():
            to_line(mine, line_send.at[zz], zz).wait_send()

        @pl.when(jnp.logical_or(zz < z, row < rows_n - 1))
        def _():
            block = block_id(row, zz, core)

            def on(r):
                @pl.when(r != cross_row)
                def _():
                    to_row(block, column_send.at[r * chips + zz], r).wait_send()

            later_rows(on)

            @pl.when(zz < z)
            def _():
                to_mate(block).wait_send()

        @pl.when(has_cross)
        def _():
            to_line(block_id(cross_row, z, core), cross_send.at[zz], zz).wait_send()

    around(sent_own)
    later_rows(lambda r: to_row(mine, column_send.at[r * chips + z], r).wait_send())

    @pl.when(core == 0)
    def _():
        to_mate(mine).wait_send()

    def sent_rows(r, _):
        def step(zz, _):
            to_mate(block_id(r, zz, core)).wait_send()
            return 0

        lax.fori_loop(0, chips, step, 0)
        return 0

    lax.fori_loop(0, row, sent_rows, 0)


def local(rows_n, line_n, queries, keys, values):
    group, tokens, head = queries.shape
    blocks = rows_n * line_n
    chips = line_n // CORES
    count = group * tokens
    return pl.pallas_call(
        functools.partial(kernel, rows_n, line_n),
        out_shape=jax.ShapeDtypeStruct(queries.shape, jnp.bfloat16),
        in_specs=[pl.BlockSpec(memory_space=pl.ANY)] * 3,
        out_specs=pl.BlockSpec(memory_space=pltpu.VMEM),
        scratch_shapes=[
            pltpu.VMEM(queries.shape, queries.dtype),
            pltpu.VMEM((blocks, 2, tokens, head), keys.dtype),
            pltpu.VMEM((count, head), jnp.float32),
            pltpu.VMEM((count, head), jnp.float32),
            pltpu.VMEM((count, head), jnp.float32),
            pltpu.SemaphoreType.DMA((3,)),
            pltpu.SemaphoreType.DMA((chips,)),
            pltpu.SemaphoreType.DMA((rows_n * chips,)),
            pltpu.SemaphoreType.DMA((chips,)),
            pltpu.SemaphoreType.DMA((blocks,)),
            pltpu.SemaphoreType.DMA((blocks,)),
        ],
        compiler_params=pltpu.CompilerParams(collective_id=0, has_side_effects=True),
    )(queries, keys, values)


def solution(mesh):
    rows_n, line_n = mesh.shape["cx"], mesh.shape["cy"]
    in_specs = (P(None, ("cx", "cy"), None), P(("cx", "cy"), None), P(("cx", "cy"), None))
    out_specs = P(None, ("cx", "cy"), None)
    return jax.shard_map(
        functools.partial(local, rows_n, line_n), mesh=mesh, in_specs=in_specs, out_specs=out_specs, check_vma=False
    )
```

time: 44.8 us -> 21.1 us (0.47)
  the two profiles are of different devices: /device:TPU:31 before, /device:TPU:7 now
where the time goes in v1:
time: 21.1 us; the launch traced here: 20.9 us
  Pallas kernels  19.3 us (91%)
  local copies, waits for them, and re-layouts  1.55 us (7%)
    pallas_call x1, Pallas kernels, local(): pl.pallas_call(functools.partial(kernel, rows_n, line_n), out_shape=jax.S...  19.3 us
    unnamed x1, local copies, waits for them, and re-layouts  1.55 us

profile of v1, /device:TPU:7, one launch (start us, length us, event | category | flops | bytes accessed | tf_op | source)
XLA Modules:
  0.0 20.9 jit_solution(8319903089825483672)
XLA Ops:
  0.0 19.3 %shard_map.37 = bf16[7,64,128]{2,1,0:T(8,128)(2,1)} custom-call(bf16[7,64,128]{2,1,0:T(8,128)(2,1)} %queries_hbm.1, bf16[64,128]{1,0:T(8,128)(2,1)} %keys_hbm.1, bf16[64,128]{1,0:T(8,128)(2,1)} %values_hbm.1), custom_call_target="tpu_custom_call" | custom-call | tf_op jit(solution)/shard_map/pallas_call | solution.py:281
  19.3 1.6 %copy.5 = bf16[7,64,128]{2,1,0:T(8,128)(2,1)} copy(bf16[7,64,128]{2,1,0:T(8,128)(2,1)} %shard_map.37) | data formatting | bytes 229376

commit v2 on v1

--- a/solution.py
+++ b/solution.py
@@ -81,7 +81,7 @@
     load_v.wait()
     pl.semaphore_wait(barrier, chips - 1 + rows_n - 1 + 1)
 
-    def around(body):
+    def around(body, first=1, last=chips):
         def step(d, _):
             @pl.when(z + d < chips)
             def _():
@@ -92,7 +92,7 @@
                 body(z - d)
             return 0
 
-        lax.fori_loop(1, chips, step, 0)
+        lax.fori_loop(first, last, step, 0)
 
     def later_rows(body):
         def step(r, _):
@@ -132,6 +132,13 @@
             low, v, preferred_element_type=jnp.float32
         )
 
+    def lane_sums(weights):
+        width = weights.shape[1]
+        if width % head:
+            lane = lax.broadcasted_iota(jnp.int32, (count, head), 1)
+            return jnp.where(lane == 0, jnp.sum(weights, axis=1, keepdims=True), 0.0)
+        return sum(weights[:, i : i + head] for i in range(0, width, head))
+
     def fold(first, blocks):
         scores = scores_of(first, blocks)
         old = peak[...]
@@ -139,7 +146,7 @@
         shrink = jnp.exp2((old - fresh) * scale)
         weights = jnp.exp2((scores - fresh[:, :1]) * scale)
         peak[...] = fresh
-        total[...] = total[...] * shrink + jnp.sum(weights, axis=1, keepdims=True)
+        total[...] = total[...] * shrink + lane_sums(weights)
         mixed[...] = mixed[...] * shrink + mix(weights, first, blocks)
 
     scores = scores_of(mine, 1)
@@ -150,7 +157,7 @@
     top = jnp.max(scores, axis=1, keepdims=True)
     weights = jnp.where(visible, jnp.exp2((scores - top) * scale), 0.0)
     peak[...] = jnp.broadcast_to(top, peak.shape)
-    total[...] = jnp.broadcast_to(jnp.sum(weights, axis=1, keepdims=True), total.shape)
+    total[...] = lane_sums(weights)
     mixed[...] = mix(weights, mine, 1)
 
     def pass_own_row(zz):
@@ -176,24 +183,27 @@
         around(lambda zz: to_line(block, cross_send.at[zz], zz).start())
         to_mate(block).start()
 
+    around(pass_own_row, 1, 2)
+
     @pl.when(has_cross)
     def _():
         pass_cross()
 
-    around(pass_own_row)
-
-    @pl.when(core == 1)
-    def _():
-        block = block_id(row, z, 0)
-        arrived(block)
-        fold(block, 1)
-
-    def own_row_step(zz, _):
-        arrived(block_id(row, zz, 1 - core))
-        fold(block_id(row, zz, 0), CORES)
-        return 0
-
-    lax.fori_loop(0, z, own_row_step, 0)
+    around(pass_own_row, 2, chips)
+
+    def fold_own_row():
+        @pl.when(core == 1)
+        def _():
+            block = block_id(row, z, 0)
+            arrived(block)
+            fold(block, 1)
+
+        def own_row_step(zz, _):
+            arrived(block_id(row, zz, 1 - core))
+            fold(block_id(row, zz, 0), CORES)
+            return 0
+
+        lax.fori_loop(0, z, own_row_step, 0)
 
     def take_row(r):
         def step(zz):
@@ -221,15 +231,29 @@
 
         lax.fori_loop(0, line_n // span, part, 0)
 
+    def row_at(i):
+        ahead = row - i
+        passed = jnp.where(ahead <= cross_row, ahead - 1, ahead)
+        return jnp.where(has_cross, jnp.where(i == 0, cross_row, passed), ahead - 1)
+
+    @pl.when(row > 0)
+    def _():
+        take_row(row_at(0))
+
+    fold_own_row()
+
     def earlier(i, _):
-        r = row - 1 - i
-        take_row(r)
-        fold_row(r)
+        take_row(row_at(i))
+        fold_row(row_at(i - 1))
         return 0
 
-    lax.fori_loop(0, row, earlier, 0)
-
-    out_ref[...] = (mixed[...] / total[...]).astype(out_ref.dtype).reshape(out_ref.shape)
+    lax.fori_loop(1, row, earlier, 0)
+
+    @pl.when(row > 0)
+    def _():
+        fold_row(row_at(row - 1))
+
+    out_ref[...] = (mixed[...] / jnp.sum(total[...], axis=1, keepdims=True)).astype(out_ref.dtype).reshape(out_ref.shape)
 
     def sent_own(zz):
         @pl.when(jnp.logical_or(zz > z, row < rows_n - 1))
@@ -280,8 +304,8 @@
     count = group * tokens
     return pl.pallas_call(
         functools.partial(kernel, rows_n, line_n),
-        out_shape=jax.ShapeDtypeStruct(queries.shape, jnp.bfloat16),
-        in_specs=[pl.BlockSpec(memory_space=pl.ANY)] * 3,
+        out_shape=pltpu.VMEM(queries.shape, jnp.bfloat16),
+        in_specs=[pl.BlockSpec(memory_space=pltpu.HBM)] * 3,
         out_specs=pl.BlockSpec(memory_space=pltpu.VMEM),
         scratch_shapes=[
             pltpu.VMEM(queries.shape, queries.dtype),

time: 21.1 us -> 18.3 us (0.87)
  Pallas kernels: 19.3 us -> 17.4 us
  local copies, waits for them, and re-layouts: 1.55 us -> 0.65 us
    pallas_call x1, Pallas kernels: 19.3 us -> 17.4 us  [local(): pl.pallas_call(functools.partial(kernel, rows_n, line_n), out_shape=pltpu...]
    unnamed x1, local copies, waits for them, and re-layouts: 1.55 us -> 0.65 us
where the time goes in v2:
time: 18.3 us; the launch traced here: 18 us
  Pallas kernels  17.4 us (95%)
  local copies, waits for them, and re-layouts  0.65 us (4%)
    pallas_call x1, Pallas kernels, local(): pl.pallas_call(functools.partial(kernel, rows_n, line_n), out_shape=pltpu...  17.4 us
    unnamed x1, local copies, waits for them, and re-layouts  0.65 us

profile of v2, /device:TPU:7, one launch (start us, length us, event | category | flops | bytes accessed | tf_op | source)
XLA Modules:
  0.0 18.0 jit_solution(14757945173754244891)
XLA Ops:
  0.0 17.4 %shard_map.37 = bf16[7,64,128]{2,1,0:T(8,128)(2,1)S(1)} custom-call(bf16[7,64,128]{2,1,0:T(8,128)(2,1)} %queries_hbm.1, bf16[64,128]{1,0:T(8,128)(2,1)} %keys_hbm.1, bf16[64,128]{1,0:T(8,128)(2,1)} %values_hbm.1), custom_call_target="tpu_custom_call" | custom-call | tf_op jit(solution)/shard_map/pallas_call | solution.py:305
  17.4 0.6 %copy.5 = bf16[7,64,128]{2,1,0:T(8,128)(2,1)} copy(bf16[7,64,128]{2,1,0:T(8,128)(2,1)S(1)} %shard_map.37) | data formatting | bytes 229376

commit v3 on v2

--- a/solution.py
+++ b/solution.py
@@ -56,27 +56,27 @@
     load_k = pltpu.make_async_copy(keys_hbm, kv.at[mine, 0], in_sems.at[0])
     load_v = pltpu.make_async_copy(values_hbm, kv.at[mine, 1], in_sems.at[1])
     load_q = pltpu.make_async_copy(queries_hbm, queries, in_sems.at[2])
+
+    barrier = pltpu.get_barrier_semaphore()
+
+    def greet_line(i, _):
+        @pl.when(i != z)
+        def _():
+            pl.semaphore_signal(barrier, inc=1, device_id=(row, place_of(i)), device_id_type=MESH)
+        return 0
+
+    def greet_column(i, _):
+        @pl.when(i != row)
+        def _():
+            pl.semaphore_signal(barrier, inc=1, device_id=(i, place), device_id_type=MESH)
+        return 0
+
+    lax.fori_loop(0, chips, greet_line, 0)
+    lax.fori_loop(0, rows_n, greet_column, 0)
+    pl.semaphore_signal(barrier, inc=1, device_id=(row, mate), device_id_type=MESH)
     load_k.start()
     load_v.start()
     load_q.start()
-
-    barrier = pltpu.get_barrier_semaphore()
-
-    def greet_line(i, _):
-        @pl.when(i != z)
-        def _():
-            pl.semaphore_signal(barrier, inc=1, device_id=(row, place_of(i)), device_id_type=MESH)
-        return 0
-
-    def greet_column(i, _):
-        @pl.when(i != row)
-        def _():
-            pl.semaphore_signal(barrier, inc=1, device_id=(i, place), device_id_type=MESH)
-        return 0
-
-    lax.fori_loop(0, chips, greet_line, 0)
-    lax.fori_loop(0, rows_n, greet_column, 0)
-    pl.semaphore_signal(barrier, inc=1, device_id=(row, mate), device_id_type=MESH)
     load_k.wait()
     load_v.wait()
     pl.semaphore_wait(barrier, chips - 1 + rows_n - 1 + 1)
@@ -94,6 +94,21 @@
 
         lax.fori_loop(first, last, step, 0)
 
+    def around_far_first(body):
+        def step(i, _):
+            d = chips - i
+
+            @pl.when(z + d < chips)
+            def _():
+                body(z + d)
+
+            @pl.when(z - d >= 0)
+            def _():
+                body(z - d)
+            return 0
+
+        lax.fori_loop(1, chips, step, 0)
+
     def later_rows(body):
         def step(r, _):
             body(r)
@@ -109,7 +124,7 @@
         def _():
             to_line(mine, line_send.at[zz], zz).start()
 
-    around(send_own)
+    around_far_first(send_own)
     later_rows(lambda r: to_row(mine, column_send.at[r * chips + z], r).start())
 
     @pl.when(core == 0)
@@ -180,7 +195,7 @@
     def pass_cross():
         block = block_id(cross_row, z, core)
         arrived(block)
-        around(lambda zz: to_line(block, cross_send.at[zz], zz).start())
+        around_far_first(lambda zz: to_line(block, cross_send.at[zz], zz).start())
         to_mate(block).start()
 
     around(pass_own_row, 1, 2)
@@ -205,53 +220,59 @@
 
         lax.fori_loop(0, z, own_row_step, 0)
 
-    def take_row(r):
+    halves = 2 if chips % 2 == 0 else 1
+    stretch = chips // halves
+    near = z // stretch
+
+    def take(r, half):
         def step(zz):
             block = block_id(r, zz, core)
             arrived(block)
             to_mate(block).start()
 
-        @pl.when(r != cross_row)
+        @pl.when(jnp.logical_and(r != cross_row, half == near))
         def _():
             step(z)
 
-        around(step)
-
-    def fold_row(r):
-        def wait_mate(zz, _):
-            arrived(block_id(r, zz, 1 - core))
-            return 0
-
-        lax.fori_loop(0, chips, wait_mate, 0)
-        span = min(SPAN, line_n)
+        def other(zz):
+            @pl.when(zz // stretch == half)
+            def _():
+                step(zz)
+
+        around(other)
+
+    def fold_half(r, half):
+        def wait_mate(i, _):
+            arrived(block_id(r, half * stretch + i, 1 - core))
+            return 0
+
+        lax.fori_loop(0, stretch, wait_mate, 0)
+        span = min(SPAN, stretch * CORES)
 
         def part(i, _):
-            fold(r * line_n + i * span, span)
-            return 0
-
-        lax.fori_loop(0, line_n // span, part, 0)
+            fold(block_id(r, half * stretch, 0) + i * span, span)
+            return 0
+
+        lax.fori_loop(0, stretch * CORES // span, part, 0)
 
     def row_at(i):
         ahead = row - i
         passed = jnp.where(ahead <= cross_row, ahead - 1, ahead)
         return jnp.where(has_cross, jnp.where(i == 0, cross_row, passed), ahead - 1)
 
-    @pl.when(row > 0)
-    def _():
-        take_row(row_at(0))
-
+    def each_row(body):
+        def step(i, _):
+            body(row_at(i))
+            return 0
+
+        lax.fori_loop(0, row, step, 0)
+
+    each_row(lambda r: take(r, near))
     fold_own_row()
-
-    def earlier(i, _):
-        take_row(row_at(i))
-        fold_row(row_at(i - 1))
-        return 0
-
-    lax.fori_loop(1, row, earlier, 0)
-
-    @pl.when(row > 0)
-    def _():
-        fold_row(row_at(row - 1))
+    each_row(lambda r: fold_half(r, near))
+    if halves == 2:
+        each_row(lambda r: take(r, 1 - near))
+        each_row(lambda r: fold_half(r, 1 - near))
 
     out_ref[...] = (mixed[...] / jnp.sum(total[...], axis=1, keepdims=True)).astype(out_ref.dtype).reshape(out_ref.shape)
 

time: 18.3 us -> 19 us (1.038)
  the two profiles are of different devices: /device:TPU:7 before, /device:TPU:31 now
where the time goes in v3:
time: 19 us; the launch traced here: 18.8 us
  Pallas kernels  18.1 us (95%)
  local copies, waits for them, and re-layouts  0.65 us (3%)
    pallas_call x1, Pallas kernels, local(): pl.pallas_call(functools.partial(kernel, rows_n, line_n), out_shape=pltpu...  18.1 us
    unnamed x1, local copies, waits for them, and re-layouts  0.65 us

profile of v3, /device:TPU:31, one launch (start us, length us, event | category | flops | bytes accessed | tf_op | source)
XLA Modules:
  0.0 18.8 jit_solution(3449774285113170044)
XLA Ops:
  0.0 18.1 %shard_map.37 = bf16[7,64,128]{2,1,0:T(8,128)(2,1)S(1)} custom-call(bf16[7,64,128]{2,1,0:T(8,128)(2,1)} %queries_hbm.1, bf16[64,128]{1,0:T(8,128)(2,1)} %keys_hbm.1, bf16[64,128]{1,0:T(8,128)(2,1)} %values_hbm.1), custom_call_target="tpu_custom_call" | custom-call | tf_op jit(solution)/shard_map/pallas_call | solution.py:326
  18.1 0.6 %copy.5 = bf16[7,64,128]{2,1,0:T(8,128)(2,1)} copy(bf16[7,64,128]{2,1,0:T(8,128)(2,1)S(1)} %shard_map.37) | data formatting | bytes 229376
